TPU v7x, 128 devices: a whole 4x4x4 slice. The times are simulated.
128 devices in a mesh: train: 8 (over z, x_hi), serve: 16 (over x_lo, y, core).
Axes of the slice: x: 4 (x_hi: 2, x_lo: 2; x = x_hi * 2 + x_lo), y: 4, z: 4, core: 2. Of those that a mesh axis runs over, the one named last changes fastest.
Arguments:
- train_weights: bfloat16 [16, 7680, 2112], P(None, 'train', 'serve'), may hold values from -6 to 6
- row_offset: int32 [16, 9], replicated, may hold values from 0 to 7168, as said below
- block_group: int32 [16, 224, 1], P(None, 'train'), may hold values from 0 to 15; in each aligned block of 28 rows (0 to 27, 28 to 55, ..., all dimensions but the last counted through in order) at most 3 rows name the same one
Outputs:
- quant_codes: bfloat16 [16, 16, 8, 3, 32, 2112], P(None, 'serve', 'train')
- block_scales: float32 [16, 16, 8, 3, 2112], P(None, 'serve', 'train')
Inputs may be any that keep to these rules, and one draw needn't show every extreme that they name: For every layer l: row_offset[l, 0] = 0 and row_offset[l, 8] = 7168; every other row_offset[l, t] lies 1 to 32 rows above or below t * 896, never on it; in every layer one entry lies exactly 32 rows above and another exactly 32 rows below; layer 1 has the opposite sign of layer 0 at every such entry. `block_group`: within each aligned block of 28 entries (one training device's blocks of one layer), no group is named more than 3 times; some group reaches 3 in some of them.
All inputs are finite; a program needn't handle non-finite values.
Results may differ from a plain program's by a relative error of at most 0.001.
Values may be sent and summed in bfloat16 or wider, within the bound.
A program may use at most 128 MiB of HBM per device.

v0:
```python
import functools

import jax
import jax.numpy as jnp
from jax import lax
from jax.experimental import pallas as pl
from jax.experimental.pallas import tpu as pltpu
from jax.sharding import PartitionSpec as P

MESH = pl.DeviceIdType.MESH
BF = jnp.bfloat16
F32 = jnp.float32
I32 = jnp.int32
LAYERS = 16
BLOCK = 32
BLOCKS_DEV = 28
HELD = BLOCKS_DEV + 2
ROWS_DEV = 896
BUFFER = HELD * BLOCK
COLS = 132
SERVE_N = 16
TRAIN_N = 8
SLOTS = 3
FEAT = SERVE_N * COLS
TILES = -(-FEAT // 128)

PARTS = (2, 4, 4, 4, 2)
FIRST = (0, 2, 6, 10, 14)
SIZES = tuple(n * SLOTS * BLOCK + 16 for n in PARTS)
BASES = tuple(sum(SIZES[:i]) for i in range(len(PARTS)))
TOTAL = sum(SIZES)
HALO = 16 + LAYERS * BLOCK
HALO_ENDS = tuple(16 + (f + n) * BLOCK for f, n in zip(FIRST, PARTS))
HALO_BASES = (0,) + HALO_ENDS[:-1]

BASE = 2
EXTRA = 8
MESSAGES = ((0, 2, 0), (2, 8, 0), (10, 4, EXTRA), (14, 2, 0))
LENGTHS = tuple((n * BASE + e) * BLOCK + 16 for _, n, e in MESSAGES)
PAIRS = LAYERS // 2
EARLY = 5
EDGE = BLOCK + LAYERS * BLOCK
HALO_STARTS = (0, 3 * BLOCK, (1 + 2 * EARLY) * BLOCK, EDGE)


def full_exchange(
    blocks_at, held, offsets, weights, out, scales,
    raw, edge, rot, lanes, tails, turned, rest, hsend, hrecv, send, recv, patch,
    raw_sem, edge_sem, hs_sem, hr_sem, s_sem, r_sem,
):
    t = lax.axis_index("train")
    me = lax.axis_index("serve")
    mx, my, mc = me // 8, lax.rem(me // 2, 4), lax.rem(me, 2)
    right, left = lax.rem(t + 1, TRAIN_N), lax.rem(t + TRAIN_N - 1, TRAIN_N)

    def peer(v):
        return (
            lax.rem(mx + v // 8, 2) * 8
            + lax.rem(my + lax.rem(v // 2, 4), 4) * 2
            + lax.rem(mc + lax.rem(v, 2), 2)
        )

    barrier = pltpu.get_barrier_semaphore()
    for v in range(1, SERVE_N):
        pl.semaphore_signal(barrier, inc=1, device_id={"serve": peer(v)}, device_id_type=MESH)
    for other in (left, right):
        pl.semaphore_signal(barrier, inc=1, device_id={"train": other}, device_id_type=MESH)

    edges = [
        pltpu.make_async_copy(weights.at[:, b], edge.at[side], edge_sem.at[side])
        for side, b in enumerate((BLOCKS_DEV + 1, 0))
    ]
    loads = [
        pltpu.make_async_copy(weights.at[pl.ds(f, n)], raw.at[pl.ds(f, n)], raw_sem.at[i])
        for i, (f, n) in enumerate(zip(FIRST, PARTS))
    ]
    for copy in edges + loads:
        copy.start()

    row = lax.broadcasted_iota(jnp.int32, (COLS, 256), 0)
    col = lax.broadcasted_iota(jnp.int32, (COLS, 256), 1)
    turn = (row < 128) & (col < 128) & (col == ((row + 4 * me) & 127))
    spread = (row >= 128) & (col >= 128) & ((col & 3) == row - 128)
    rot[...] = jnp.where(turn | spread, 1.0, 0.0).astype(BF)
    lane16 = lax.broadcasted_iota(jnp.int32, (16, 128), 1)
    for m in range(32):
        lanes[m] = jnp.where((lane16 >> 2) == m, 1.0, 0.0).astype(BF)
    rrow = lax.broadcasted_iota(jnp.int32, (128, 128), 0)
    rcol = lax.broadcasted_iota(jnp.int32, (128, 128), 1)
    patch[...] = jnp.where((rrow & 3) == (rcol & 3), 1.0, 0.0).astype(BF)

    for copy in edges:
        copy.wait()
    for side in range(2):
        def edge_step(i, total, side=side):
            x = edge[side, pl.ds(i * 4, 4)].reshape(4 * BLOCK, COLS)
            y = jnp.dot(x, rot[...], preferred_element_type=F32).astype(BF)
            hsend[side, pl.ds(pl.multiple_of(16 + i * 128, 16), 128)] = y[:, :128]
            for q in range(8):
                total = total + y[q * 16 : q * 16 + 16, 128:] * lanes[lax.rem(i * 8 + q + me, 32)]
            return total

        hsend[side, 0:16] = lax.fori_loop(0, LAYERS // 4, edge_step, jnp.zeros((16, 128), BF))

    pl.semaphore_wait(barrier, SERVE_N + 1)

    halos = []
    for i in range(len(PARTS)):
        window = pl.ds(HALO_BASES[i], HALO_ENDS[i] - HALO_BASES[i])
        for side, target in enumerate((right, left)):
            copy = pltpu.make_async_remote_copy(
                src_ref=hsend.at[side, window],
                dst_ref=hrecv.at[side, window],
                send_sem=hs_sem.at[side, i],
                recv_sem=hr_sem.at[side, i],
                device_id={"train": target},
                device_id_type=MESH,
            )
            copy.start()
            halos.append(copy)

    def block_copy(i, v):
        window = pl.ds(BASES[i], SIZES[i])
        return pltpu.make_async_remote_copy(
            src_ref=send.at[v, window],
            dst_ref=recv.at[me, window],
            send_sem=s_sem.at[i, v],
            recv_sem=r_sem.at[i, v],
            device_id={"serve": peer(v)},
            device_id_type=MESH,
        )

    block_row = lax.broadcasted_iota(jnp.int32, (BLOCK, 128), 0)

    for i, (f, n) in enumerate(zip(FIRST, PARTS)):
        loads[i].wait()

        def turn_step(j, carry, f=f):
            l, b = j // 7, lax.rem(j, 7) * 4
            x = raw[f + l, pl.ds(b + 1, 4)].reshape(4 * BLOCK, COLS)
            y = jnp.dot(x, rot[...], preferred_element_type=F32).astype(BF)
            turned[l, pl.ds(b, 4)] = y[:, :128].reshape(4, BLOCK, 128)
            rest[l, pl.ds(b, 4)] = y[:, 128:].reshape(4, BLOCK, 128)
            return carry

        lax.fori_loop(0, n * 7, turn_step, 0)
        halos[2 * i].wait_recv()
        halos[2 * i + 1].wait_recv()

        def patch_step(l, carry, f=f):
            layer = f + l
            first = offsets[layer, t] - t * ROWS_DEV
            last = offsets[layer, t + 1] - t * ROWS_DEV - (ROWS_DEV - BLOCK)
            for side, (b, take) in enumerate(
                ((0, block_row < first), (BLOCKS_DEV - 1, block_row >= last))
            ):
                main = hrecv[side, pl.ds(pl.multiple_of(16 + layer * BLOCK, 16), BLOCK)]
                packed = hrecv[side, 0:16]
                both = jnp.concatenate(
                    [packed * lanes[lax.rem(2 * layer + h + me, 32)] for h in range(2)], axis=0
                )
                tail = jnp.dot(both, patch[...], preferred_element_type=F32)
                turned[l, b] = jnp.where(take, main.astype(F32), turned[l, b].astype(F32)).astype(BF)
                rest[l, b] = jnp.where(take, tail, rest[l, b].astype(F32)).astype(BF)
            return carry

        lax.fori_loop(0, n, patch_step, 0)

        def fill(dest, index, group, i=i, f=f, n=n):
            total = jnp.zeros((16, 128), BF)
            for l in range(n):
                for k in range(SLOTS):
                    slot = l * SLOTS + k
                    b = blocks_at[f + l, group * SLOTS + k]
                    dest[index, pl.ds(BASES[i] + slot * BLOCK, BLOCK)] = turned[l, b]
                    pair = rest[l, b]
                    for h in range(2):
                        total = total + pair[h * 16 : h * 16 + 16] * lanes[
                            lax.rem(2 * slot + h + me, 32)
                        ]
            dest[index, pl.ds(BASES[i] + n * SLOTS * BLOCK, 16)] = total

        def send_step(j, carry, i=i, fill=fill):
            v = SERVE_N - 1 - j
            fill(send, v, peer(v))
            block_copy(i, v).start()
            return carry

        lax.fori_loop(0, SERVE_N - 1, send_step, 0)
        fill(recv, me, me)

    lane = lax.broadcasted_iota(jnp.int32, (BLOCK, 128), 1)
    for i, (f, n) in enumerate(zip(FIRST, PARTS)):
        def arrive(j, carry, i=i):
            block_copy(i, j + 1).wait_recv()
            return carry

        lax.fori_loop(0, SERVE_N - 1, arrive, 0)

        def tail_step(q, carry, i=i, n=n):
            total = jnp.zeros((16, 128), BF)
            for s in range(SERVE_N):
                total = total + recv[s, pl.ds(BASES[i] + n * SLOTS * BLOCK, 16)] * lanes[
                    lax.rem(q + s, 32)
                ]
            tails[q // 2, pl.ds(pl.multiple_of(lax.rem(q, 2) * 16, 16), 16)] = pltpu.roll(
                total.astype(F32), 128 - 4 * q, axis=1
            )
            return carry

        lax.fori_loop(0, 2 * n * SLOTS, tail_step, 0)

        def block_step(slot, carry, i=i, f=f):
            layer, k = f + slot // SLOTS, lax.rem(slot, SLOTS)
            there = held[layer, me * SLOTS + k].astype(F32)
            at = f * SLOTS + slot
            tail = tails[slot]
            before = None
            for j in range(TILES):
                if j < SERVE_N:
                    now = recv[j, pl.ds(pl.multiple_of(BASES[i] + slot * BLOCK, 16), BLOCK)].astype(F32)
                else:
                    now = tail
                if j == 0:
                    value = now
                else:
                    value = jnp.where(
                        lane < 4 * j - 4, before, jnp.where(lane < 4 * j, tail, now)
                    )
                before = now
                top = jnp.maximum(jnp.max(jnp.abs(value), axis=0, keepdims=True), 0.25)
                codes = (value * (there / top)).astype(BF)
                width = min(128, FEAT - j * 128)
                out[at, :, j * 128 : j * 128 + width] = codes[:, :width]
                scales[at, :, j * 128 : j * 128 + width] = (top * there)[:, :width]
            return carry

        lax.fori_loop(0, n * SLOTS, block_step, 0)

    for copy in halos:
        copy.wait_send()
    for i in range(len(PARTS)):
        def leave(j, carry, i=i):
            block_copy(i, j + 1).wait_send()
            return carry

        lax.fori_loop(0, SERVE_N - 1, leave, 0)


def route(
    groups, offsets, weights, out, scales, flag,
    named, found, table, raw, eye, spread, turning, mixed_tail, lanes, turned, rest,
    hsend, hrecv, tails, extra_codes, extra_scales, fsend, frecv,
    send0, send1, send2, send3, recv0, recv1, recv2, recv3,
    table_sem, raw_sem, hs_sem, hr_sem, s_sem, r_sem, fs_sem, fr_sem,
):
    sends, recvs = (send0, send1, send2, send3), (recv0, recv1, recv2, recv3)
    t = lax.axis_index("train")
    me = lax.axis_index("serve")
    mx, my, mc = me // 8, lax.rem(me // 2, 4), lax.rem(me, 2)
    right, left = lax.rem(t + 1, TRAIN_N), lax.rem(t + TRAIN_N - 1, TRAIN_N)

    def peer(v):
        return (
            lax.rem(mx + v // 8, 2) * 8
            + lax.rem(my + lax.rem(v // 2, 4), 4) * 2
            + lax.rem(mc + lax.rem(v, 2), 2)
        )

    barrier = pltpu.get_barrier_semaphore()
    for v in range(1, SERVE_N):
        pl.semaphore_signal(barrier, inc=1, device_id={"serve": peer(v)}, device_id_type=MESH)
    for step in range(1, TRAIN_N):
        pl.semaphore_signal(
            barrier, inc=1, device_id={"train": lax.rem(t + step, TRAIN_N)}, device_id_type=MESH
        )

    def load(m, rows=16):
        return pltpu.make_async_copy(
            weights.at[pl.ds(16 * m, rows)], raw.at[pl.ds(16 + 16 * m, rows)], raw_sem.at[m]
        )

    wrapped = pltpu.make_async_copy(weights.at[112:128], raw.at[0:16], raw_sem.at[9])
    wrapped.start()
    for m in range(8):
        load(m).start()
    load(8, 4).start()

    def index(shape, dim):
        return lax.broadcasted_iota(I32, shape, dim)

    def ones(cond):
        return jnp.where(cond, 1.0, 0.0).astype(BF)

    lane16, row16 = index((16, 128), 1), index((16, 128), 0)
    named[...] = jnp.full((16, 128), -1, I32)
    named[:, 0:BLOCKS_DEV] = groups[...]
    group = named[...]
    order = jnp.zeros((16, 128), I32)
    for d in range(1, BLOCKS_DEV):
        same = (pltpu.roll(group, d, axis=1) == group) & (lane16 >= d)
        order = order + jnp.where(same, 1, 0)
    slot_of = group * SLOTS + order
    blocks_at = jnp.zeros((16, 128), I32)
    third_at = jnp.zeros((16, 128), I32)
    counted = jnp.zeros((16, 128), I32)
    for b in range(BLOCKS_DEV):
        slot_b = slot_of[:, b : b + 1]
        blocks_at = jnp.where(slot_b == lane16, b, blocks_at)
        third_at = jnp.where(slot_b == lane16 * SLOTS + BASE, b, third_at)
        counted = counted + jnp.where(group[:, b : b + 1] == lane16, 1, 0)
    third = jnp.where(counted > BASE, 1, 0)
    before = jnp.zeros((16, 128), I32)
    for d in range(1, LAYERS):
        before = before + jnp.where(row16 >= d, pltpu.roll(third, d, axis=0), 0)
    found[0:16] = blocks_at
    found[16:32] = counted
    found[32:48] = jnp.minimum(before, EXTRA - 1)
    where_third = row16 * HELD + 1 + third_at
    for e in range(EXTRA):
        mine = (third > 0) & (before == e)
        found[48 + e : 49 + e] = jnp.sum(jnp.where(mine, where_third, 0), axis=0, keepdims=True)
    known = pltpu.make_async_copy(found, table, table_sem)
    known.start()
    long = jnp.where(jnp.sum(third, axis=0, keepdims=True) > EXTRA, 1.0, 0.0)
    fsend[...] = jnp.broadcast_to(long, (8, 128))
    frecv[t] = fsend[...]

    eye[...] = ones(index((256, 256), 0) == index((256, 256), 1))
    a, b = index((256, 256), 0), index((256, 256), 1)
    spread[...] = ones(((b >> 4) == (a & 15)) & ((b & 15) == (a >> 4)))
    for m in range(32):
        lanes[m] = ones((lane16 >> 2) == m)

    NT = (((1,), (1,)), ((), ()))

    def gather_columns(m, tiles):
        start = 16 * (m + 1) - 4 * lax.rem(me, 4)
        place = 16 * lax.rem(m + me // 4, 8)
        for r, w in tiles:
            x = raw[pl.ds(start, 16), :, r : r + w].reshape(256, w)
            y = jnp.dot(spread[...], x, preferred_element_type=F32).astype(BF)
            for layer in range(LAYERS):
                window = pl.ds(pl.multiple_of(128 * layer + place, 16), 16)
                turning[window, r : r + w] = y[16 * layer : 16 * layer + 16]

    ends, middle = ((0, 128), (896, 64)), ((128, 256), (384, 256), (640, 256))
    wrapped.wait()

    def ends_step(m, carry):
        load(m).wait()
        gather_columns(m, ends)
        return carry

    lax.fori_loop(0, 8, ends_step, 0)
    load(8, 4).wait()

    def turn_tail(tiles):
        for r, w in tiles:
            x = raw[144:148, :, r : r + w].reshape(64, w)
            y = lax.dot_general(eye[:w, :w], x, NT, preferred_element_type=F32)
            mixed_tail[r : r + w] = y.astype(BF)

    turn_tail(ends)
    hsend[0, 0:BLOCK, 0:64] = mixed_tail[BUFFER - BLOCK : BUFFER]
    hsend[1, 0:BLOCK, 0:64] = mixed_tail[0:BLOCK]
    hsend[0, 0:BLOCK, 64:128] = jnp.zeros((BLOCK, 64), BF)
    hsend[1, 0:BLOCK, 64:128] = jnp.zeros((BLOCK, 64), BF)

    def edge_step(p, carry):
        rows = pl.ds(pl.multiple_of(256 * p, 256), 256)
        low = lax.dot_general(eye[0:32, 0:128], turning[rows, 0:128], NT, preferred_element_type=F32)
        high = lax.dot_general(
            eye[32:64, 0:64], turning[rows, 896:960], NT, preferred_element_type=F32
        )
        for h in range(2):
            window = pl.ds(pl.multiple_of(BLOCK + (2 * p + h) * BLOCK, BLOCK), BLOCK)
            hsend[0, window] = high[:, 128 * h : 128 * h + 128].astype(BF)
            hsend[1, window] = low[:, 128 * h : 128 * h + 128].astype(BF)
        return carry

    lax.fori_loop(0, PAIRS, edge_step, 0, unroll=2)

    def middle_step(m, carry):
        gather_columns(m, middle)
        return carry

    def tail_pick(p):
        k, q = index((64, 256), 0), index((64, 256), 1)
        return ones(((k & 15) == 2 * p + (q >> 7)) & ((k >> 4) == (q & 3)))

    def prepare_step(p, carry):
        rows = pl.ds(pl.multiple_of(256 * p, 256), 256)
        tail_of = tail_pick(p)
        for r, w in ((0, 128), (128, 256), (384, 256), (640, 256), (896, 64)):
            y = lax.dot_general(
                eye[:w, :w], turning[rows, r : r + w], NT, preferred_element_type=F32
            ).astype(BF)
            z = jnp.dot(mixed_tail[r : r + w], tail_of, preferred_element_type=F32).astype(BF)
            for h in range(2):
                at = pl.ds((2 * p + h) * HELD + r // BLOCK, w // BLOCK)
                turned[at] = y[:, 128 * h : 128 * h + 128].reshape(w // BLOCK, BLOCK, 128)
                rest[at] = z[:, 128 * h : 128 * h + 128].reshape(w // BLOCK, BLOCK, 128)
        return carry

    def halo(side, i):
        window = pl.ds(HALO_STARTS[i], HALO_STARTS[i + 1] - HALO_STARTS[i])
        return pltpu.make_async_remote_copy(
            src_ref=hsend.at[side, window],
            dst_ref=hrecv.at[side, window],
            send_sem=hs_sem.at[side, i],
            recv_sem=hr_sem.at[side, i],
            device_id={"train": (right, left)[side]},
            device_id_type=MESH,
        )

    block_row = index((BLOCK, 128), 0)

    def patch(p):
        tail_of = tail_pick(p)
        for side, (b, last) in enumerate(((1, False), (HELD - 2, True))):
            tail = jnp.dot(hrecv[side, 0:BLOCK, 0:64], tail_of, preferred_element_type=F32)
            for h in range(2):
                layer = 2 * p + h
                if last:
                    take = block_row >= offsets[layer, t + 1] - t * ROWS_DEV - (ROWS_DEV - BLOCK)
                else:
                    take = block_row < offsets[layer, t] - t * ROWS_DEV
                at = layer * HELD + b
                window = pl.ds(pl.multiple_of(BLOCK + layer * BLOCK, BLOCK), BLOCK)
                main = hrecv[side, window].astype(F32)
                turned[at] = jnp.where(take, main, turned[at].astype(F32)).astype(BF)
                rest[at] = jnp.where(
                    take, tail[:, 128 * h : 128 * h + 128], rest[at].astype(F32)
                ).astype(BF)

    def patch_step(p, carry):
        patch(p)
        return carry

    def message(i, v):
        return pltpu.make_async_remote_copy(
            src_ref=sends[i].at[v],
            dst_ref=recvs[i].at[me],
            send_sem=s_sem.at[i, v],
            recv_sem=r_sem.at[i, v],
            device_id={"serve": peer(v)},
            device_id_type=MESH,
        )

    def dispatch(i):
        f, n, e = MESSAGES[i]

        def fill(dest, place, group):
            total = jnp.zeros((16, 128), BF)
            for slot in range(n * BASE + e):
                if slot < n * BASE:
                    layer, k = f + slot // BASE, slot % BASE
                    at = layer * HELD + 1 + table[layer, group * SLOTS + k]
                else:
                    at = table[48 + slot - n * BASE, group]
                dest[place, slot * BLOCK : slot * BLOCK + BLOCK] = turned[at]
                pair = rest[at]
                for h in range(2):
                    mask = lanes[lax.rem(2 * slot + h + me, 32)]
                    total = total + pair[h * 16 : h * 16 + 16] * mask
            dest[place, LENGTHS[i] - 16 : LENGTHS[i]] = total

        def send_step(j, carry):
            v = SERVE_N - 1 - j
            fill(sends[i], v, peer(v))
            message(i, v).start()
            return carry

        lax.fori_loop(0, SERVE_N - 1, send_step, 0)
        fill(recvs[i], me, me)

    lane = index((BLOCK, 128), 1)

    def finish(i):
        f, n, e = MESSAGES[i]
        recv = recvs[i]

        def arrive(j, carry):
            message(i, j + 1).wait_recv()
            return carry

        lax.fori_loop(0, SERVE_N - 1, arrive, 0)

        def tail_step(q, carry):
            total = jnp.zeros((16, 128), BF)
            for s in range(SERVE_N):
                total = total + recv[s, LENGTHS[i] - 16 : LENGTHS[i]] * lanes[lax.rem(q + s, 32)]
            tails[q // 2, pl.ds(pl.multiple_of(lax.rem(q, 2) * 16, 16), 16)] = pltpu.roll(
                total.astype(F32), 128 - 4 * q, axis=1
            )
            return carry

        lax.fori_loop(0, 2 * (n * BASE + e), tail_step, 0)

        def scale_block(slot, at, there, codes_out, scales_out):
            tail = tails[slot]
            before = None
            for j in range(TILES):
                if j < SERVE_N:
                    now = recv[j, pl.ds(pl.multiple_of(slot * BLOCK, BLOCK), BLOCK)].astype(F32)
                else:
                    now = tail
                if j == 0:
                    value = now
                else:
                    value = jnp.where(
                        lane < 4 * j - 4, before, jnp.where(lane < 4 * j, tail, now)
                    )
                before = now
                top = jnp.maximum(jnp.max(jnp.abs(value), axis=0, keepdims=True), 0.25)
                codes = (value * (there / top)).astype(BF)
                width = min(128, FEAT - j * 128)
                codes_out[at, :, j * 128 : j * 128 + width] = codes[:, :width]
                scales_out[at, :, j * 128 : j * 128 + width] = (top * there)[:, :width]

        def present(layer, k):
            return jnp.minimum(jnp.maximum(table[16 + layer, me] - k, 0), 1).astype(F32)

        def base_step(slot, carry):
            layer, k = f + slot // BASE, lax.rem(slot, BASE)
            scale_block(slot, layer * SLOTS + k, present(layer, k), out, scales)
            return carry

        lax.fori_loop(0, n * BASE, base_step, 0)
        if e:
            def extra_step(entry, carry):
                scale_block(n * BASE + entry, entry, 1.0, extra_codes, extra_scales)
                return carry

            lax.fori_loop(0, e, extra_step, 0)

            def place_step(layer, carry):
                entry, there = table[32 + layer, me], present(layer, BASE)
                at = layer * SLOTS + BASE
                out[at] = (extra_codes[entry].astype(F32) * there).astype(BF)
                scales[at] = extra_scales[entry] * there
                return carry

            lax.fori_loop(0, LAYERS, place_step, 0)

    def tell(step):
        return pltpu.make_async_remote_copy(
            src_ref=fsend,
            dst_ref=frecv.at[t],
            send_sem=fs_sem.at[step],
            recv_sem=fr_sem.at[step],
            device_id={"train": lax.rem(t + step, TRAIN_N)},
            device_id_type=MESH,
        )

    pl.semaphore_wait(barrier, SERVE_N + TRAIN_N - 2)
    for i in range(3):
        for side in range(2):
            halo(side, i).start()
    for step in range(1, TRAIN_N):
        tell(step).start()
    lax.fori_loop(0, 8, middle_step, 0)
    turn_tail(middle)
    lax.fori_loop(0, 1, prepare_step, 0)
    known.wait()
    for side in range(2):
        halo(side, 0).wait_recv()
    patch(0)
    dispatch(0)
    lax.fori_loop(1, EARLY, prepare_step, 0)
    for side in range(2):
        halo(side, 1).wait_recv()
    lax.fori_loop(1, EARLY, patch_step, 0)
    dispatch(1)
    lax.fori_loop(EARLY, PAIRS, prepare_step, 0)
    for side in range(2):
        halo(side, 2).wait_recv()
    lax.fori_loop(EARLY, PAIRS, patch_step, 0)
    dispatch(2)
    dispatch(3)
    finish(0)
    finish(1)
    finish(2)
    finish(3)
    for step in range(1, TRAIN_N):
        tell(step).wait()
    flag[...] = jnp.broadcast_to(jnp.max(frecv[...]).reshape(1, 1), (8, 128))

    for side in range(2):
        halo(side, 0).wait_send()
        halo(side, 1).wait_send()
        halo(side, 2).wait_send()
    for i in range(len(MESSAGES)):
        def leave(j, carry, i=i):
            message(i, j + 1).wait_send()
            return carry

        lax.fori_loop(0, SERVE_N - 1, leave, 0)


def everything(train_weights, row_offset, groups):
    position = jnp.arange(BLOCKS_DEV, dtype=I32)
    earlier = position[None, :] < position[:, None]
    same = groups[:, :, None] == groups[:, None, :]
    order = jnp.sum((same & earlier[None]).astype(I32), axis=2)
    slot_id = groups * SLOTS + order
    onehot = slot_id[:, None, :] == jnp.arange(SERVE_N * SLOTS, dtype=I32)[None, :, None]
    blocks_at = jnp.sum(jnp.where(onehot, position[None, None, :], 0), axis=2)
    group_ids = jnp.arange(SERVE_N, dtype=I32)
    counts = jnp.sum((groups[:, None, :] == group_ids[None, :, None]).astype(I32), axis=2)
    held = (counts[:, :, None] > jnp.arange(SLOTS, dtype=I32)).astype(I32)
    held = held.reshape(LAYERS, SERVE_N * SLOTS)
    weights = train_weights.reshape(LAYERS, HELD, BLOCK, COLS)
    parts = len(PARTS)
    smem = pl.BlockSpec(memory_space=pltpu.SMEM)
    vmem = pl.BlockSpec(memory_space=pltpu.VMEM)
    return pl.pallas_call(
        full_exchange,
        out_shape=(
            pltpu.VMEM((LAYERS * SLOTS, BLOCK, FEAT), BF),
            pltpu.VMEM((LAYERS * SLOTS, 1, FEAT), F32),
        ),
        in_specs=[smem, smem, smem, pl.BlockSpec(memory_space=pl.ANY)],
        out_specs=(vmem, vmem),
        scratch_shapes=[
            pltpu.VMEM((LAYERS, HELD, BLOCK, COLS), BF),
            pltpu.VMEM((2, LAYERS, BLOCK, COLS), BF),
            pltpu.VMEM((COLS, 256), BF),
            pltpu.VMEM((32, 16, 128), BF),
            pltpu.VMEM((max(PARTS) * SLOTS, BLOCK, 128), F32),
            pltpu.VMEM((max(PARTS), BLOCKS_DEV, BLOCK, 128), BF),
            pltpu.VMEM((max(PARTS), BLOCKS_DEV, BLOCK, 128), BF),
            pltpu.VMEM((2, HALO, 128), BF),
            pltpu.VMEM((2, HALO, 128), BF),
            pltpu.VMEM((SERVE_N, TOTAL, 128), BF),
            pltpu.VMEM((SERVE_N, TOTAL, 128), BF),
            pltpu.VMEM((128, 128), BF),
            pltpu.SemaphoreType.DMA((parts,)),
            pltpu.SemaphoreType.DMA((2,)),
            pltpu.SemaphoreType.DMA((2, parts)),
            pltpu.SemaphoreType.DMA((2, parts)),
            pltpu.SemaphoreType.DMA((parts, SERVE_N)),
            pltpu.SemaphoreType.DMA((parts, SERVE_N)),
        ],
        compiler_params=pltpu.CompilerParams(
            collective_id=1, has_side_effects=True, vmem_limit_bytes=44 * 2**20
        ),
    )(blocks_at, held, row_offset, weights)


def shards(train_weights, row_offset, block_group):
    groups = block_group[:, :, 0]
    smem = pl.BlockSpec(memory_space=pltpu.SMEM)
    vmem = pl.BlockSpec(memory_space=pltpu.VMEM)
    parts = len(MESSAGES)
    codes, scales, flag = pl.pallas_call(
        route,
        out_shape=(
            pltpu.VMEM((LAYERS * SLOTS, BLOCK, FEAT), BF),
            pltpu.VMEM((LAYERS * SLOTS, 1, FEAT), F32),
            jax.ShapeDtypeStruct((8, 128), F32),
        ),
        in_specs=[vmem, smem, pl.BlockSpec(memory_space=pl.ANY)],
        out_specs=(vmem, vmem, vmem),
        scratch_shapes=[
            pltpu.VMEM((LAYERS, 128), I32),
            pltpu.VMEM((56, 128), I32),
            pltpu.SMEM((56, 128), I32),
            pltpu.VMEM((COLS + 16, LAYERS, BUFFER), BF),
            pltpu.VMEM((256, 256), BF),
            pltpu.VMEM((256, 256), BF),
            pltpu.VMEM((128 * LAYERS, BUFFER), BF),
            pltpu.VMEM((BUFFER, 64), BF),
            pltpu.VMEM((32, 16, 128), BF),
            pltpu.VMEM((LAYERS * HELD, BLOCK, 128), BF),
            pltpu.VMEM((LAYERS * HELD, BLOCK, 128), BF),
            pltpu.VMEM((2, EDGE, 128), BF),
            pltpu.VMEM((2, EDGE, 128), BF),
            pltpu.VMEM((16, BLOCK, 128), F32),
            pltpu.VMEM((EXTRA, BLOCK, FEAT), BF),
            pltpu.VMEM((EXTRA, 1, FEAT), F32),
            pltpu.VMEM((8, 128), F32),
            pltpu.VMEM((TRAIN_N, 8, 128), F32),
            *[pltpu.VMEM((SERVE_N, length, 128), BF) for length in LENGTHS * 2],
            pltpu.SemaphoreType.DMA,
            pltpu.SemaphoreType.DMA((10,)),
            pltpu.SemaphoreType.DMA((2, 3)),
            pltpu.SemaphoreType.DMA((2, 3)),
            pltpu.SemaphoreType.DMA((parts, SERVE_N)),
            pltpu.SemaphoreType.DMA((parts, SERVE_N)),
            pltpu.SemaphoreType.DMA((TRAIN_N,)),
            pltpu.SemaphoreType.DMA((TRAIN_N,)),
        ],
        compiler_params=pltpu.CompilerParams(
            collective_id=2, has_side_effects=True, vmem_limit_bytes=46 * 2**20
        ),
    )(
        groups, row_offset, jnp.transpose(train_weights, (2, 0, 1)),
    )
    codes, scales = lax.cond(
        flag[0, 0] > 0.0,
        lambda: tuple(everything(train_weights, row_offset, groups)),
        lambda: (codes, scales),
    )
    return (
        codes.reshape(LAYERS, 1, 1, SLOTS, BLOCK, FEAT),
        scales.reshape(LAYERS, 1, 1, SLOTS, FEAT),
    )


def solution(mesh):
    return jax.shard_map(
        shards,
        mesh=mesh,
        in_specs=(P(None, "train", "serve"), P(), P(None, "train", None)),
        out_specs=(P(None, "serve", "train", None, None, None), P(None, "serve", "train", None, None)),
        check_vma=False,
    )
```

profile of v0, /device:TPU:1, one launch (start us, length us, event | category | flops | bytes accessed | tf_op | source)
XLA Modules:
  0.0 85.2 jit_solution(13450649034078060702)
XLA Ops:
  0.6 79.8 %shard_map.50 = (bf16[48,32,2112]{2,1,0:T(8,128)(2,1)S(1)}, f32[48,1,2112]{2,1,0:T(1,128)S(1)}, f32[8,128]{1,0:T(8,128)S(1)}) custom-call(s32[16,28]{1,0:T(8,128)} %bitcast.18, s32[16,9]{1,0:T(8,128)} %offsets.1, bf16[132,16,960]{2,1,0:T(8,128)(2,1)} %bitcast.17), custom_call_target="tpu_custom_call" | custom-call | tf_op jit(solution)/shard_map/pallas_call | solution.py:657
  80.4 0.5 slice.3
  81.6 2.8 %copy.22 = bf16[16,1,1,3,32,2112]{5,4,3,2,1,0:T(8,128)(2,1)} copy(bf16[16,1,1,3,32,2112]{5,4,3,2,1,0:T(8,128)(2,1)S(1)} %get-tuple-element.60) | data formatting | bytes 12976128
  84.4 0.8 copy.23
  (1 shorter events, 0.0 us)
where the time goes:
time: 86.8 us; the launch traced here: 85.2 us
  Pallas kernels  79.8 us (92%)
  local copies, waits for them, and re-layouts  4.1 us (5%)
  between operations  1.3 us (1%)
    pallas_call x1, Pallas kernels, shards(): pl.pallas_call(route, out_shape=(pltpu.VMEM((LAYERS * SLOTS, BLOCK, FEAT)...  79.8 us
    unnamed x2, local copies, waits for them, and re-layouts  3.59 us

commit v1 on v0

--- a/solution.py
+++ b/solution.py
@@ -35,8 +35,9 @@
 
 BASE = 2
 EXTRA = 8
-MESSAGES = ((0, 2, 0), (2, 8, 0), (10, 4, EXTRA), (14, 2, 0))
-LENGTHS = tuple((n * BASE + e) * BLOCK + 16 for _, n, e in MESSAGES)
+MESSAGES = ((0, 2, 2), (2, 8, 8), (10, 4, 6), (14, 2, 0))
+LENGTHS = tuple(n * BASE * BLOCK + (16 if m else 0) for _, n, m in MESSAGES)
+LIST = EXTRA * BLOCK + 16
 PAIRS = LAYERS // 2
 EARLY = 5
 EDGE = BLOCK + LAYERS * BLOCK
@@ -248,11 +249,11 @@
 
 
 def route(
-    groups, offsets, weights, out, scales, flag,
-    named, found, table, raw, eye, spread, turning, mixed_tail, lanes, turned, rest,
+    groups_in, offsets_in, weights, out, scales, flag,
+    groups, offsets, named, found, table, raw, eye, spread, turning, mixed_tail, lanes, turned, rest,
     hsend, hrecv, tails, extra_codes, extra_scales, fsend, frecv,
-    send0, send1, send2, send3, recv0, recv1, recv2, recv3,
-    table_sem, raw_sem, hs_sem, hr_sem, s_sem, r_sem, fs_sem, fr_sem,
+    send0, send1, send2, send3, recv0, recv1, recv2, recv3, lists,
+    small_sem, table_sem, raw_sem, hs_sem, hr_sem, s_sem, r_sem, ls_sem, lr_sem, fs_sem, fr_sem,
 ):
     sends, recvs = (send0, send1, send2, send3), (recv0, recv1, recv2, recv3)
     t = lax.axis_index("train")
@@ -267,6 +268,22 @@
             + lax.rem(mc + lax.rem(v, 2), 2)
         )
 
+    small = [
+        pltpu.make_async_copy(groups_in, groups, small_sem.at[0]),
+        pltpu.make_async_copy(offsets_in, offsets, small_sem.at[1]),
+    ]
+    loads = [
+        [
+            pltpu.make_async_copy(
+                weights.at[a : a + n, :, r : r + w], raw.at[b : b + n, :, r : r + w], raw_sem.at[i, j]
+            )
+            for j, (a, b, n) in enumerate(((0, 16, COLS), (112, 0, 16)))
+        ]
+        for i, (r, w) in enumerate(((0, 128), (896, 64), (128, 768)))
+    ]
+    for copy in loads[0] + loads[1] + small + loads[2]:
+        copy.start()
+
     barrier = pltpu.get_barrier_semaphore()
     for v in range(1, SERVE_N):
         pl.semaphore_signal(barrier, inc=1, device_id={"serve": peer(v)}, device_id_type=MESH)
@@ -275,17 +292,6 @@
             barrier, inc=1, device_id={"train": lax.rem(t + step, TRAIN_N)}, device_id_type=MESH
         )
 
-    def load(m, rows=16):
-        return pltpu.make_async_copy(
-            weights.at[pl.ds(16 * m, rows)], raw.at[pl.ds(16 + 16 * m, rows)], raw_sem.at[m]
-        )
-
-    wrapped = pltpu.make_async_copy(weights.at[112:128], raw.at[0:16], raw_sem.at[9])
-    wrapped.start()
-    for m in range(8):
-        load(m).start()
-    load(8, 4).start()
-
     def index(shape, dim):
         return lax.broadcasted_iota(I32, shape, dim)
 
@@ -293,6 +299,274 @@
         return jnp.where(cond, 1.0, 0.0).astype(BF)
 
     lane16, row16 = index((16, 128), 1), index((16, 128), 0)
+    eye[...] = ones(index((256, 256), 0) == index((256, 256), 1))
+    a, b = index((256, 256), 0), index((256, 256), 1)
+    spread[...] = ones(((b >> 4) == (a & 15)) & ((b & 15) == (a >> 4)))
+    for m in range(32):
+        lanes[m] = ones((lane16 >> 2) == m)
+
+    NT = (((1,), (1,)), ((), ()))
+
+    def gather_columns(m, tiles):
+        start = 16 * (m + 1) - 4 * lax.rem(me, 4)
+        place = 16 * lax.rem(m + me // 4, 8)
+        for r, w in tiles:
+            x = raw[pl.ds(start, 16), :, r : r + w].reshape(256, w)
+            y = jnp.dot(spread[...], x, preferred_element_type=F32).astype(BF)
+            for layer in range(LAYERS):
+                window = pl.ds(pl.multiple_of(128 * layer + place, 16), 16)
+                turning[window, r : r + w] = y[16 * layer : 16 * layer + 16]
+
+    ends, middle = ((0, 128), (896, 64)), ((128, 256), (384, 256), (640, 256))
+    for copy in loads[0] + loads[1]:
+        copy.wait()
+    for m in range(8):
+        gather_columns(m, ends)
+
+    def turn_tail(tiles):
+        for r, w in tiles:
+            x = raw[144:148, :, r : r + w].reshape(64, w)
+            y = lax.dot_general(eye[:w, :w], x, NT, preferred_element_type=F32)
+            mixed_tail[r : r + w] = y.astype(BF)
+
+    turn_tail(ends)
+    hsend[0, 0:BLOCK, 0:64] = mixed_tail[BUFFER - BLOCK : BUFFER]
+    hsend[1, 0:BLOCK, 0:64] = mixed_tail[0:BLOCK]
+    hsend[0, 0:BLOCK, 64:128] = jnp.zeros((BLOCK, 64), BF)
+    hsend[1, 0:BLOCK, 64:128] = jnp.zeros((BLOCK, 64), BF)
+
+    def edge_step(p, carry):
+        rows = pl.ds(pl.multiple_of(256 * p, 256), 256)
+        low = lax.dot_general(eye[0:32, 0:128], turning[rows, 0:128], NT, preferred_element_type=F32)
+        high = lax.dot_general(
+            eye[32:64, 0:64], turning[rows, 896:960], NT, preferred_element_type=F32
+        )
+        for h in range(2):
+            window = pl.ds(pl.multiple_of(BLOCK + (2 * p + h) * BLOCK, BLOCK), BLOCK)
+            hsend[0, window] = high[:, 128 * h : 128 * h + 128].astype(BF)
+            hsend[1, window] = low[:, 128 * h : 128 * h + 128].astype(BF)
+        return carry
+
+    lax.fori_loop(0, PAIRS, edge_step, 0, unroll=8)
+
+    def tail_pick(p):
+        k, q = index((64, 256), 0), index((64, 256), 1)
+        return ones(((k & 15) == 2 * p + (q >> 7)) & ((k >> 4) == (q & 3)))
+
+    def prepare_step(p, carry):
+        rows = pl.ds(pl.multiple_of(256 * p, 256), 256)
+        tail_of = tail_pick(p)
+        for r, w in ((0, 128), (128, 256), (384, 256), (640, 256), (896, 64)):
+            y = lax.dot_general(
+                eye[:w, :w], turning[rows, r : r + w], NT, preferred_element_type=F32
+            ).astype(BF)
+            z = jnp.dot(mixed_tail[r : r + w], tail_of, preferred_element_type=F32).astype(BF)
+            for h in range(2):
+                at = pl.ds((2 * p + h) * HELD + r // BLOCK, w // BLOCK)
+                turned[at] = y[:, 128 * h : 128 * h + 128].reshape(w // BLOCK, BLOCK, 128)
+                rest[at] = z[:, 128 * h : 128 * h + 128].reshape(w // BLOCK, BLOCK, 128)
+        return carry
+
+    def halo(side, i):
+        window = pl.ds(HALO_STARTS[i], HALO_STARTS[i + 1] - HALO_STARTS[i])
+        return pltpu.make_async_remote_copy(
+            src_ref=hsend.at[side, window],
+            dst_ref=hrecv.at[side, window],
+            send_sem=hs_sem.at[side, i],
+            recv_sem=hr_sem.at[side, i],
+            device_id={"train": (right, left)[side]},
+            device_id_type=MESH,
+        )
+
+    block_row = index((BLOCK, 128), 0)
+
+    def patch(p):
+        tail_of = tail_pick(p)
+        for side, (b, last) in enumerate(((1, False), (HELD - 2, True))):
+            tail = jnp.dot(hrecv[side, 0:BLOCK, 0:64], tail_of, preferred_element_type=F32)
+            for h in range(2):
+                layer = 2 * p + h
+                if last:
+                    take = block_row >= offsets[layer, t + 1] - t * ROWS_DEV - (ROWS_DEV - BLOCK)
+                else:
+                    take = block_row < offsets[layer, t] - t * ROWS_DEV
+                at = layer * HELD + b
+                window = pl.ds(pl.multiple_of(BLOCK + layer * BLOCK, BLOCK), BLOCK)
+                main = hrecv[side, window].astype(F32)
+                turned[at] = jnp.where(take, main, turned[at].astype(F32)).astype(BF)
+                rest[at] = jnp.where(
+                    take, tail[:, 128 * h : 128 * h + 128], rest[at].astype(F32)
+                ).astype(BF)
+
+    def patch_step(p, carry):
+        patch(p)
+        return carry
+
+    def message(i, v):
+        return pltpu.make_async_remote_copy(
+            src_ref=sends[i].at[v],
+            dst_ref=recvs[i].at[me],
+            send_sem=s_sem.at[i, v],
+            recv_sem=r_sem.at[i, v],
+            device_id={"serve": peer(v)},
+            device_id_type=MESH,
+        )
+
+    def tail_of_block(total, at, slot):
+        pair = rest[at]
+        for h in range(2):
+            total = total + pair[h * 16 : h * 16 + 16] * lanes[lax.rem(2 * slot + h + me, 32)]
+        return total
+
+    def dispatch(i):
+        f, n, ends_n = MESSAGES[i]
+
+        def fill(dest, place, group):
+            total = jnp.zeros((16, 128), BF)
+            for slot in range(max(n, ends_n) * BASE):
+                layer, k = f + slot // BASE, slot % BASE
+                at = layer * HELD + 1 + table[layer, group * SLOTS + k]
+                if slot < n * BASE:
+                    dest[place, slot * BLOCK : slot * BLOCK + BLOCK] = turned[at]
+                if ends_n:
+                    total = tail_of_block(total, at, slot)
+            if ends_n:
+                dest[place, LENGTHS[i] - 16 : LENGTHS[i]] = total
+
+        def send_step(j, carry):
+            v = SERVE_N - 1 - j
+            fill(sends[i], v, peer(v))
+            message(i, v).start()
+            return carry
+
+        lax.fori_loop(0, SERVE_N - 1, send_step, 0)
+        fill(recvs[i], me, me)
+
+    own_list, next_list = mc * 8 + mx * 4 + my, mc * 8 + (1 - mx) * 4 + my
+
+    def list_copy(i):
+        if i == 0:
+            window, target = pl.ds(own_list, 1), (1 - mx) * 8 + my * 2 + mc
+        elif i < 4:
+            window, target = pl.ds(own_list, 1), mx * 8 + lax.rem(my + i, 4) * 2 + mc
+        elif i < 7:
+            window, target = pl.ds(next_list, 1), mx * 8 + lax.rem(my + i - 3, 4) * 2 + mc
+        else:
+            window, target = pl.ds(8 * mc, 8), mx * 8 + my * 2 + 1 - mc
+        return pltpu.make_async_remote_copy(
+            src_ref=lists.at[window],
+            dst_ref=lists.at[window],
+            send_sem=ls_sem.at[i],
+            recv_sem=lr_sem.at[i],
+            device_id={"serve": target},
+            device_id_type=MESH,
+        )
+
+    def dispatch_list():
+        total = jnp.zeros((16, 128), BF)
+        for e in range(EXTRA):
+            at = table[48 + e, 0]
+            lists[own_list, e * BLOCK : e * BLOCK + BLOCK] = turned[at]
+            total = tail_of_block(total, at, e)
+        lists[own_list, LIST - 16 : LIST] = total
+        for i in range(4):
+            list_copy(i).start()
+
+    lane = index((BLOCK, 128), 1)
+
+    def take_tails(recv, rows, count, base):
+        def tail_step(q, carry):
+            total = jnp.zeros((16, 128), BF)
+            for s in range(SERVE_N):
+                total = total + recv[place_of(recv, s), rows] * lanes[lax.rem(q + s, 32)]
+            tails[base + q // 2, pl.ds(pl.multiple_of(lax.rem(q, 2) * 16, 16), 16)] = pltpu.roll(
+                total.astype(F32), 128 - 4 * q, axis=1
+            )
+            return carry
+
+        lax.fori_loop(0, 2 * count, tail_step, 0)
+
+    def place_of(recv, s):
+        return s % 2 * 8 + s // 8 * 4 + s // 2 % 4 if recv is lists else s
+
+    def scale_block(recv, slot, tail, at, there, codes_out, scales_out):
+        before = None
+        for j in range(TILES):
+            if j < SERVE_N:
+                window = pl.ds(pl.multiple_of(slot * BLOCK, BLOCK), BLOCK)
+                now = recv[place_of(recv, j), window].astype(F32)
+            else:
+                now = tail
+            if j == 0:
+                value = now
+            else:
+                value = jnp.where(lane < 4 * j - 4, before, jnp.where(lane < 4 * j, tail, now))
+            before = now
+            top = jnp.maximum(jnp.max(jnp.abs(value), axis=0, keepdims=True), 0.25)
+            codes = (value * (there / top)).astype(BF)
+            width = min(128, FEAT - j * 128)
+            codes_out[at, :, j * 128 : j * 128 + width] = codes[:, :width]
+            scales_out[at, :, j * 128 : j * 128 + width] = (top * there)[:, :width]
+
+    def present(layer, k):
+        return jnp.minimum(jnp.maximum(table[16 + layer, me] - k, 0), 1).astype(F32)
+
+    def finish(i):
+        f, n, ends_n = MESSAGES[i]
+
+        def arrive(j, carry):
+            message(i, j + 1).wait_recv()
+            return carry
+
+        lax.fori_loop(0, SERVE_N - 1, arrive, 0)
+        if ends_n:
+            take_tails(recvs[i], slice(LENGTHS[i] - 16, LENGTHS[i]), ends_n * BASE, 0)
+        past = 0 if ends_n else (f - MESSAGES[i - 1][0]) * BASE
+
+        def base_step(slot, carry):
+            layer, k = f + slot // BASE, lax.rem(slot, BASE)
+            scale_block(
+                recvs[i], slot, tails[past + slot], layer * SLOTS + k, present(layer, k), out, scales
+            )
+            return carry
+
+        lax.fori_loop(0, n * BASE, base_step, 0)
+
+    def finish_list():
+        list_copy(7).wait_recv()
+        take_tails(lists, slice(LIST - 16, LIST), EXTRA, 16)
+
+        def extra_step(entry, carry):
+            scale_block(lists, entry, tails[16 + entry], entry, 1.0, extra_codes, extra_scales)
+            return carry
+
+        lax.fori_loop(0, EXTRA, extra_step, 0)
+
+        def place_step(layer, carry):
+            entry, there = table[32 + layer, me], present(layer, BASE)
+            at = layer * SLOTS + BASE
+            out[at] = (extra_codes[entry].astype(F32) * there).astype(BF)
+            scales[at] = extra_scales[entry] * there
+            return carry
+
+        lax.fori_loop(0, LAYERS, place_step, 0)
+
+    def tell(step):
+        return pltpu.make_async_remote_copy(
+            src_ref=fsend,
+            dst_ref=frecv.at[t],
+            send_sem=fs_sem.at[step],
+            recv_sem=fr_sem.at[step],
+            device_id={"train": lax.rem(t + step, TRAIN_N)},
+            device_id_type=MESH,
+        )
+
+    pl.semaphore_wait(barrier, SERVE_N + TRAIN_N - 2)
+    for i in range(3):
+        for side in range(2):
+            halo(side, i).start()
+    for copy in small:
+        copy.wait()
     named[...] = jnp.full((16, 128), -1, I32)
     named[:, 0:BLOCKS_DEV] = groups[...]
     group = named[...]
@@ -310,257 +584,34 @@
         third_at = jnp.where(slot_b == lane16 * SLOTS + BASE, b, third_at)
         counted = counted + jnp.where(group[:, b : b + 1] == lane16, 1, 0)
     third = jnp.where(counted > BASE, 1, 0)
+    rows_third = jnp.broadcast_to(jnp.sum(third, axis=1, keepdims=True), (16, 128))
     before = jnp.zeros((16, 128), I32)
     for d in range(1, LAYERS):
-        before = before + jnp.where(row16 >= d, pltpu.roll(third, d, axis=0), 0)
+        before = before + jnp.where(row16 >= d, pltpu.roll(rows_third, d, axis=0), 0)
+        before = before + jnp.where(lane16 >= d, pltpu.roll(third, d, axis=1), 0)
     found[0:16] = blocks_at
     found[16:32] = counted
     found[32:48] = jnp.minimum(before, EXTRA - 1)
     where_third = row16 * HELD + 1 + third_at
+
+    def whole(x):
+        return jnp.sum(jnp.sum(x, axis=0, keepdims=True), axis=1, keepdims=True)
+
     for e in range(EXTRA):
         mine = (third > 0) & (before == e)
-        found[48 + e : 49 + e] = jnp.sum(jnp.where(mine, where_third, 0), axis=0, keepdims=True)
+        found[48 + e : 49 + e] = jnp.broadcast_to(whole(jnp.where(mine, where_third, 0)), (1, 128))
     known = pltpu.make_async_copy(found, table, table_sem)
     known.start()
-    long = jnp.where(jnp.sum(third, axis=0, keepdims=True) > EXTRA, 1.0, 0.0)
+    long = jnp.where(whole(third) > EXTRA, 1.0, 0.0)
     fsend[...] = jnp.broadcast_to(long, (8, 128))
     frecv[t] = fsend[...]
 
-    eye[...] = ones(index((256, 256), 0) == index((256, 256), 1))
-    a, b = index((256, 256), 0), index((256, 256), 1)
-    spread[...] = ones(((b >> 4) == (a & 15)) & ((b & 15) == (a >> 4)))
-    for m in range(32):
-        lanes[m] = ones((lane16 >> 2) == m)
-
-    NT = (((1,), (1,)), ((), ()))
-
-    def gather_columns(m, tiles):
-        start = 16 * (m + 1) - 4 * lax.rem(me, 4)
-        place = 16 * lax.rem(m + me // 4, 8)
-        for r, w in tiles:
-            x = raw[pl.ds(start, 16), :, r : r + w].reshape(256, w)
-            y = jnp.dot(spread[...], x, preferred_element_type=F32).astype(BF)
-            for layer in range(LAYERS):
-                window = pl.ds(pl.multiple_of(128 * layer + place, 16), 16)
-                turning[window, r : r + w] = y[16 * layer : 16 * layer + 16]
-
-    ends, middle = ((0, 128), (896, 64)), ((128, 256), (384, 256), (640, 256))
-    wrapped.wait()
-
-    def ends_step(m, carry):
-        load(m).wait()
-        gather_columns(m, ends)
-        return carry
-
-    lax.fori_loop(0, 8, ends_step, 0)
-    load(8, 4).wait()
-
-    def turn_tail(tiles):
-        for r, w in tiles:
-            x = raw[144:148, :, r : r + w].reshape(64, w)
-            y = lax.dot_general(eye[:w, :w], x, NT, preferred_element_type=F32)
-            mixed_tail[r : r + w] = y.astype(BF)
-
-    turn_tail(ends)
-    hsend[0, 0:BLOCK, 0:64] = mixed_tail[BUFFER - BLOCK : BUFFER]
-    hsend[1, 0:BLOCK, 0:64] = mixed_tail[0:BLOCK]
-    hsend[0, 0:BLOCK, 64:128] = jnp.zeros((BLOCK, 64), BF)
-    hsend[1, 0:BLOCK, 64:128] = jnp.zeros((BLOCK, 64), BF)
-
-    def edge_step(p, carry):
-        rows = pl.ds(pl.multiple_of(256 * p, 256), 256)
-        low = lax.dot_general(eye[0:32, 0:128], turning[rows, 0:128], NT, preferred_element_type=F32)
-        high = lax.dot_general(
-            eye[32:64, 0:64], turning[rows, 896:960], NT, preferred_element_type=F32
-        )
-        for h in range(2):
-            window = pl.ds(pl.multiple_of(BLOCK + (2 * p + h) * BLOCK, BLOCK), BLOCK)
-            hsend[0, window] = high[:, 128 * h : 128 * h + 128].astype(BF)
-            hsend[1, window] = low[:, 128 * h : 128 * h + 128].astype(BF)
-        return carry
-
-    lax.fori_loop(0, PAIRS, edge_step, 0, unroll=2)
-
-    def middle_step(m, carry):
-        gather_columns(m, middle)
-        return carry
-
-    def tail_pick(p):
-        k, q = index((64, 256), 0), index((64, 256), 1)
-        return ones(((k & 15) == 2 * p + (q >> 7)) & ((k >> 4) == (q & 3)))
-
-    def prepare_step(p, carry):
-        rows = pl.ds(pl.multiple_of(256 * p, 256), 256)
-        tail_of = tail_pick(p)
-        for r, w in ((0, 128), (128, 256), (384, 256), (640, 256), (896, 64)):
-            y = lax.dot_general(
-                eye[:w, :w], turning[rows, r : r + w], NT, preferred_element_type=F32
-            ).astype(BF)
-            z = jnp.dot(mixed_tail[r : r + w], tail_of, preferred_element_type=F32).astype(BF)
-            for h in range(2):
-                at = pl.ds((2 * p + h) * HELD + r // BLOCK, w // BLOCK)
-                turned[at] = y[:, 128 * h : 128 * h + 128].reshape(w // BLOCK, BLOCK, 128)
-                rest[at] = z[:, 128 * h : 128 * h + 128].reshape(w // BLOCK, BLOCK, 128)
-        return carry
-
-    def halo(side, i):
-        window = pl.ds(HALO_STARTS[i], HALO_STARTS[i + 1] - HALO_STARTS[i])
-        return pltpu.make_async_remote_copy(
-            src_ref=hsend.at[side, window],
-            dst_ref=hrecv.at[side, window],
-            send_sem=hs_sem.at[side, i],
-            recv_sem=hr_sem.at[side, i],
-            device_id={"train": (right, left)[side]},
-            device_id_type=MESH,
-        )
-
-    block_row = index((BLOCK, 128), 0)
-
-    def patch(p):
-        tail_of = tail_pick(p)
-        for side, (b, last) in enumerate(((1, False), (HELD - 2, True))):
-            tail = jnp.dot(hrecv[side, 0:BLOCK, 0:64], tail_of, preferred_element_type=F32)
-            for h in range(2):
-                layer = 2 * p + h
-                if last:
-                    take = block_row >= offsets[layer, t + 1] - t * ROWS_DEV - (ROWS_DEV - BLOCK)
-                else:
-                    take = block_row < offsets[layer, t] - t * ROWS_DEV
-                at = layer * HELD + b
-                window = pl.ds(pl.multiple_of(BLOCK + layer * BLOCK, BLOCK), BLOCK)
-                main = hrecv[side, window].astype(F32)
-                turned[at] = jnp.where(take, main, turned[at].astype(F32)).astype(BF)
-                rest[at] = jnp.where(
-                    take, tail[:, 128 * h : 128 * h + 128], rest[at].astype(F32)
-                ).astype(BF)
-
-    def patch_step(p, carry):
-        patch(p)
-        return carry
-
-    def message(i, v):
-        return pltpu.make_async_remote_copy(
-            src_ref=sends[i].at[v],
-            dst_ref=recvs[i].at[me],
-            send_sem=s_sem.at[i, v],
-            recv_sem=r_sem.at[i, v],
-            device_id={"serve": peer(v)},
-            device_id_type=MESH,
-        )
-
-    def dispatch(i):
-        f, n, e = MESSAGES[i]
-
-        def fill(dest, place, group):
-            total = jnp.zeros((16, 128), BF)
-            for slot in range(n * BASE + e):
-                if slot < n * BASE:
-                    layer, k = f + slot // BASE, slot % BASE
-                    at = layer * HELD + 1 + table[layer, group * SLOTS + k]
-                else:
-                    at = table[48 + slot - n * BASE, group]
-                dest[place, slot * BLOCK : slot * BLOCK + BLOCK] = turned[at]
-                pair = rest[at]
-                for h in range(2):
-                    mask = lanes[lax.rem(2 * slot + h + me, 32)]
-                    total = total + pair[h * 16 : h * 16 + 16] * mask
-            dest[place, LENGTHS[i] - 16 : LENGTHS[i]] = total
-
-        def send_step(j, carry):
-            v = SERVE_N - 1 - j
-            fill(sends[i], v, peer(v))
-            message(i, v).start()
-            return carry
-
-        lax.fori_loop(0, SERVE_N - 1, send_step, 0)
-        fill(recvs[i], me, me)
-
-    lane = index((BLOCK, 128), 1)
-
-    def finish(i):
-        f, n, e = MESSAGES[i]
-        recv = recvs[i]
-
-        def arrive(j, carry):
-            message(i, j + 1).wait_recv()
-            return carry
-
-        lax.fori_loop(0, SERVE_N - 1, arrive, 0)
-
-        def tail_step(q, carry):
-            total = jnp.zeros((16, 128), BF)
-            for s in range(SERVE_N):
-                total = total + recv[s, LENGTHS[i] - 16 : LENGTHS[i]] * lanes[lax.rem(q + s, 32)]
-            tails[q // 2, pl.ds(pl.multiple_of(lax.rem(q, 2) * 16, 16), 16)] = pltpu.roll(
-                total.astype(F32), 128 - 4 * q, axis=1
-            )
-            return carry
-
-        lax.fori_loop(0, 2 * (n * BASE + e), tail_step, 0)
-
-        def scale_block(slot, at, there, codes_out, scales_out):
-            tail = tails[slot]
-            before = None
-            for j in range(TILES):
-                if j < SERVE_N:
-                    now = recv[j, pl.ds(pl.multiple_of(slot * BLOCK, BLOCK), BLOCK)].astype(F32)
-                else:
-                    now = tail
-                if j == 0:
-                    value = now
-                else:
-                    value = jnp.where(
-                        lane < 4 * j - 4, before, jnp.where(lane < 4 * j, tail, now)
-                    )
-                before = now
-                top = jnp.maximum(jnp.max(jnp.abs(value), axis=0, keepdims=True), 0.25)
-                codes = (value * (there / top)).astype(BF)
-                width = min(128, FEAT - j * 128)
-                codes_out[at, :, j * 128 : j * 128 + width] = codes[:, :width]
-                scales_out[at, :, j * 128 : j * 128 + width] = (top * there)[:, :width]
-
-        def present(layer, k):
-            return jnp.minimum(jnp.maximum(table[16 + layer, me] - k, 0), 1).astype(F32)
-
-        def base_step(slot, carry):
-            layer, k = f + slot // BASE, lax.rem(slot, BASE)
-            scale_block(slot, layer * SLOTS + k, present(layer, k), out, scales)
-            return carry
-
-        lax.fori_loop(0, n * BASE, base_step, 0)
-        if e:
-            def extra_step(entry, carry):
-                scale_block(n * BASE + entry, entry, 1.0, extra_codes, extra_scales)
-                return carry
-
-            lax.fori_loop(0, e, extra_step, 0)
-
-            def place_step(layer, carry):
-                entry, there = table[32 + layer, me], present(layer, BASE)
-                at = layer * SLOTS + BASE
-                out[at] = (extra_codes[entry].astype(F32) * there).astype(BF)
-                scales[at] = extra_scales[entry] * there
-                return carry
-
-            lax.fori_loop(0, LAYERS, place_step, 0)
-
-    def tell(step):
-        return pltpu.make_async_remote_copy(
-            src_ref=fsend,
-            dst_ref=frecv.at[t],
-            send_sem=fs_sem.at[step],
-            recv_sem=fr_sem.at[step],
-            device_id={"train": lax.rem(t + step, TRAIN_N)},
-            device_id_type=MESH,
-        )
-
-    pl.semaphore_wait(barrier, SERVE_N + TRAIN_N - 2)
-    for i in range(3):
-        for side in range(2):
-            halo(side, i).start()
     for step in range(1, TRAIN_N):
         tell(step).start()
-    lax.fori_loop(0, 8, middle_step, 0)
+    for copy in loads[2]:
+        copy.wait()
+    for m in range(8):
+        gather_columns(m, middle)
     turn_tail(middle)
     lax.fori_loop(0, 1, prepare_step, 0)
     known.wait()
@@ -568,21 +619,28 @@
         halo(side, 0).wait_recv()
     patch(0)
     dispatch(0)
-    lax.fori_loop(1, EARLY, prepare_step, 0)
+    lax.fori_loop(1, PAIRS, prepare_step, 0, unroll=7)
     for side in range(2):
         halo(side, 1).wait_recv()
-    lax.fori_loop(1, EARLY, patch_step, 0)
+        halo(side, 2).wait_recv()
+    lax.fori_loop(1, PAIRS, patch_step, 0)
+    dispatch_list()
     dispatch(1)
-    lax.fori_loop(EARLY, PAIRS, prepare_step, 0)
-    for side in range(2):
-        halo(side, 2).wait_recv()
-    lax.fori_loop(EARLY, PAIRS, patch_step, 0)
+    finish(0)
+    list_copy(0).wait_recv()
+    for i in range(4, 7):
+        list_copy(i).start()
     dispatch(2)
     dispatch(3)
-    finish(0)
     finish(1)
+    for i in range(1, 7):
+        list_copy(i).wait_recv()
+    list_copy(7).start()
+    finish_list()
     finish(2)
     finish(3)
+    for i in range(8):
+        list_copy(i).wait_send()
     for step in range(1, TRAIN_N):
         tell(step).wait()
     flag[...] = jnp.broadcast_to(jnp.max(frecv[...]).reshape(1, 1), (8, 128))
@@ -661,9 +719,11 @@
             pltpu.VMEM((LAYERS * SLOTS, 1, FEAT), F32),
             jax.ShapeDtypeStruct((8, 128), F32),
         ),
-        in_specs=[vmem, smem, pl.BlockSpec(memory_space=pl.ANY)],
+        in_specs=[pl.BlockSpec(memory_space=pl.ANY)] * 3,
         out_specs=(vmem, vmem, vmem),
         scratch_shapes=[
+            pltpu.VMEM((LAYERS, BLOCKS_DEV), I32),
+            pltpu.SMEM((LAYERS, TRAIN_N + 1), I32),
             pltpu.VMEM((LAYERS, 128), I32),
             pltpu.VMEM((56, 128), I32),
             pltpu.SMEM((56, 128), I32),
@@ -677,18 +737,22 @@
             pltpu.VMEM((LAYERS * HELD, BLOCK, 128), BF),
             pltpu.VMEM((2, EDGE, 128), BF),
             pltpu.VMEM((2, EDGE, 128), BF),
-            pltpu.VMEM((16, BLOCK, 128), F32),
+            pltpu.VMEM((16 + EXTRA, BLOCK, 128), F32),
             pltpu.VMEM((EXTRA, BLOCK, FEAT), BF),
             pltpu.VMEM((EXTRA, 1, FEAT), F32),
             pltpu.VMEM((8, 128), F32),
             pltpu.VMEM((TRAIN_N, 8, 128), F32),
             *[pltpu.VMEM((SERVE_N, length, 128), BF) for length in LENGTHS * 2],
+            pltpu.VMEM((SERVE_N, LIST, 128), BF),
+            pltpu.SemaphoreType.DMA((2,)),
             pltpu.SemaphoreType.DMA,
-            pltpu.SemaphoreType.DMA((10,)),
+            pltpu.SemaphoreType.DMA((3, 3)),
             pltpu.SemaphoreType.DMA((2, 3)),
             pltpu.SemaphoreType.DMA((2, 3)),
             pltpu.SemaphoreType.DMA((parts, SERVE_N)),
             pltpu.SemaphoreType.DMA((parts, SERVE_N)),
+            pltpu.SemaphoreType.DMA((8,)),
+            pltpu.SemaphoreType.DMA((8,)),
             pltpu.SemaphoreType.DMA((TRAIN_N,)),
             pltpu.SemaphoreType.DMA((TRAIN_N,)),
         ],

time: 86.8 us -> 78.4 us (0.903)
  Pallas kernels: 79.8 us -> 71.7 us
    pallas_call x1, Pallas kernels: 79.8 us -> 71.7 us  [shards(): pl.pallas_call(route, out_shape=(pltpu.VMEM((LAYERS * SLOTS, BLOCK, FEAT)...]
where the time goes in v1:
time: 78.4 us; the launch traced here: 77.1 us
  Pallas kernels  71.7 us (91%)
  local copies, waits for them, and re-layouts  4.1 us (5%)
  between operations  1.3 us (2%)
    pallas_call x1, Pallas kernels, shards(): pl.pallas_call(route, out_shape=(pltpu.VMEM((LAYERS * SLOTS, BLOCK, FEAT)...  71.7 us
    unnamed x2, local copies, waits for them, and re-layouts  3.59 us

profile of v1, /device:TPU:1, one launch (start us, length us, event | category | flops | bytes accessed | tf_op | source)
XLA Modules:
  0.0 77.1 jit_solution(1551091498206747727)
XLA Ops:
  0.6 71.7 %shard_map.50 = (bf16[48,32,2112]{2,1,0:T(8,128)(2,1)S(1)}, f32[48,1,2112]{2,1,0:T(1,128)S(1)}, f32[8,128]{1,0:T(8,128)S(1)}) custom-call(s32[16,28]{1,0:T(8,128)} %bitcast.18, s32[16,9]{1,0:T(8,128)} %offsets_in.1, bf16[132,16,960]{2,1,0:T(8,128)(2,1)} %bitcast.17), custom_call_target="tpu_custom_call" | custom-call | tf_op jit(solution)/shard_map/pallas_call | solution.py:715
  72.4 0.5 slice.3
  73.6 2.8 %copy.22 = bf16[16,1,1,3,32,2112]{5,4,3,2,1,0:T(8,128)(2,1)} copy(bf16[16,1,1,3,32,2112]{5,4,3,2,1,0:T(8,128)(2,1)S(1)} %get-tuple-element.60) | data formatting | bytes 12976128
  76.4 0.8 copy.23
  (1 shorter events, 0.0 us)

commit v2 on v1

--- a/solution.py
+++ b/solution.py
@@ -35,8 +35,17 @@
 
 BASE = 2
 EXTRA = 8
-MESSAGES = ((0, 2, 2), (2, 8, 8), (10, 4, 6), (14, 2, 0))
+MESSAGES = (
+    (0, 2, ()),
+    (2, 3, tuple(range(2, 10))),
+    (5, 5, ()),
+    (10, 4, tuple(range(10, 16)) + (0, 1)),
+    (14, 2, ()),
+)
 LENGTHS = tuple(n * BASE * BLOCK + (16 if m else 0) for _, n, m in MESSAGES)
+TAIL_AT = tuple(
+    next(m.index(f) * BASE for _, _, m in MESSAGES if f in m) for f, _, _ in MESSAGES
+)
 LIST = EXTRA * BLOCK + 16
 PAIRS = LAYERS // 2
 EARLY = 5
@@ -252,10 +261,11 @@
     groups_in, offsets_in, weights, out, scales, flag,
     groups, offsets, named, found, table, raw, eye, spread, turning, mixed_tail, lanes, turned, rest,
     hsend, hrecv, tails, extra_codes, extra_scales, fsend, frecv,
-    send0, send1, send2, send3, recv0, recv1, recv2, recv3, lists,
+    send0, send1, send2, send3, send4, recv0, recv1, recv2, recv3, recv4, lists,
     small_sem, table_sem, raw_sem, hs_sem, hr_sem, s_sem, r_sem, ls_sem, lr_sem, fs_sem, fr_sem,
 ):
-    sends, recvs = (send0, send1, send2, send3), (recv0, recv1, recv2, recv3)
+    sends = (send0, send1, send2, send3, send4)
+    recvs = (recv0, recv1, recv2, recv3, recv4)
     t = lax.axis_index("train")
     me = lax.axis_index("serve")
     mx, my, mc = me // 8, lax.rem(me // 2, 4), lax.rem(me, 2)
@@ -367,12 +377,20 @@
                 rest[at] = z[:, 128 * h : 128 * h + 128].reshape(w // BLOCK, BLOCK, 128)
         return carry
 
+    has_next = (t < TRAIN_N - 1, t > 0)
+
+    def halo_arrived(i):
+        for side in range(2):
+            @pl.when(has_next[1 - side])
+            def _(side=side):
+                halo(side, i).wait_recv()
+
     def halo(side, i):
         window = pl.ds(HALO_STARTS[i], HALO_STARTS[i + 1] - HALO_STARTS[i])
         return pltpu.make_async_remote_copy(
             src_ref=hsend.at[side, window],
             dst_ref=hrecv.at[side, window],
-            send_sem=hs_sem.at[side, i],
+            send_sem=hs_sem.at[side],
             recv_sem=hr_sem.at[side, i],
             device_id={"train": (right, left)[side]},
             device_id_type=MESH,
@@ -406,8 +424,8 @@
         return pltpu.make_async_remote_copy(
             src_ref=sends[i].at[v],
             dst_ref=recvs[i].at[me],
-            send_sem=s_sem.at[i, v],
-            recv_sem=r_sem.at[i, v],
+            send_sem=s_sem.at[i],
+            recv_sem=r_sem.at[i],
             device_id={"serve": peer(v)},
             device_id_type=MESH,
         )
@@ -418,19 +436,31 @@
             total = total + pair[h * 16 : h * 16 + 16] * lanes[lax.rem(2 * slot + h + me, 32)]
         return total
 
+    def all_messages(i):
+        most = pl.ds(0, SERVE_N - 1)
+        return pltpu.make_async_remote_copy(
+            src_ref=sends[i].at[most],
+            dst_ref=recvs[i].at[most],
+            send_sem=s_sem.at[i],
+            recv_sem=r_sem.at[i],
+            device_id={"serve": peer(1)},
+            device_id_type=MESH,
+        )
+
     def dispatch(i):
-        f, n, ends_n = MESSAGES[i]
+        f, n, ends_at = MESSAGES[i]
 
         def fill(dest, place, group):
-            total = jnp.zeros((16, 128), BF)
-            for slot in range(max(n, ends_n) * BASE):
+            for slot in range(n * BASE):
                 layer, k = f + slot // BASE, slot % BASE
                 at = layer * HELD + 1 + table[layer, group * SLOTS + k]
-                if slot < n * BASE:
-                    dest[place, slot * BLOCK : slot * BLOCK + BLOCK] = turned[at]
-                if ends_n:
+                dest[place, slot * BLOCK : slot * BLOCK + BLOCK] = turned[at]
+            if ends_at:
+                total = jnp.zeros((16, 128), BF)
+                for slot in range(len(ends_at) * BASE):
+                    layer, k = ends_at[slot // BASE], slot % BASE
+                    at = layer * HELD + 1 + table[layer, group * SLOTS + k]
                     total = tail_of_block(total, at, slot)
-            if ends_n:
                 dest[place, LENGTHS[i] - 16 : LENGTHS[i]] = total
 
         def send_step(j, carry):
@@ -442,23 +472,36 @@
         lax.fori_loop(0, SERVE_N - 1, send_step, 0)
         fill(recvs[i], me, me)
 
-    own_list, next_list = mc * 8 + mx * 4 + my, mc * 8 + (1 - mx) * 4 + my
+    def list_of(dx, dy):
+        return mc * 8 + lax.rem(mx + dx, 2) * 4 + lax.rem(my + dy, 4)
 
     def list_copy(i):
-        if i == 0:
-            window, target = pl.ds(own_list, 1), (1 - mx) * 8 + my * 2 + mc
-        elif i < 4:
-            window, target = pl.ds(own_list, 1), mx * 8 + lax.rem(my + i, 4) * 2 + mc
-        elif i < 7:
-            window, target = pl.ds(next_list, 1), mx * 8 + lax.rem(my + i - 3, 4) * 2 + mc
-        else:
-            window, target = pl.ds(8 * mc, 8), mx * 8 + my * 2 + 1 - mc
+        lists_at, dx, dy, dc = (
+            (pl.ds(list_of(0, 0), 1), 1, 0, 0),
+            (pl.ds(list_of(0, 0), 1), 0, 1, 0),
+            (pl.ds(list_of(0, 0), 1), 0, 3, 0),
+            (pl.ds(list_of(0, 3), 1), 0, 1, 0),
+            (pl.ds(list_of(1, 0), 1), 0, 1, 0),
+            (pl.ds(list_of(1, 0), 1), 0, 3, 0),
+            (pl.ds(list_of(0, 2), 1), 1, 0, 0),
+            (pl.ds(8 * mc, 8), 0, 0, 1),
+        )[i]
         return pltpu.make_async_remote_copy(
-            src_ref=lists.at[window],
-            dst_ref=lists.at[window],
-            send_sem=ls_sem.at[i],
-            recv_sem=lr_sem.at[i],
-            device_id={"serve": target},
+            src_ref=lists.at[lists_at],
+            dst_ref=lists.at[lists_at],
+            send_sem=ls_sem,
+            recv_sem=lr_sem.at[(0, 1, 4, 2, 4, 4, 4, 3)[i]],
+            device_id={"serve": peer(8 * dx + 2 * dy + dc)},
+            device_id_type=MESH,
+        )
+
+    def some_lists(n):
+        return pltpu.make_async_remote_copy(
+            src_ref=lists.at[pl.ds(0, n)],
+            dst_ref=lists.at[pl.ds(0, n)],
+            send_sem=ls_sem,
+            recv_sem=lr_sem.at[4],
+            device_id={"serve": peer(1)},
             device_id_type=MESH,
         )
 
@@ -466,10 +509,10 @@
         total = jnp.zeros((16, 128), BF)
         for e in range(EXTRA):
             at = table[48 + e, 0]
-            lists[own_list, e * BLOCK : e * BLOCK + BLOCK] = turned[at]
+            lists[list_of(0, 0), e * BLOCK : e * BLOCK + BLOCK] = turned[at]
             total = tail_of_block(total, at, e)
-        lists[own_list, LIST - 16 : LIST] = total
-        for i in range(4):
+        lists[list_of(0, 0), LIST - 16 : LIST] = total
+        for i in range(3):
             list_copy(i).start()
 
     lane = index((BLOCK, 128), 1)
@@ -511,22 +554,20 @@
     def present(layer, k):
         return jnp.minimum(jnp.maximum(table[16 + layer, me] - k, 0), 1).astype(F32)
 
-    def finish(i):
-        f, n, ends_n = MESSAGES[i]
-
-        def arrive(j, carry):
-            message(i, j + 1).wait_recv()
-            return carry
-
-        lax.fori_loop(0, SERVE_N - 1, arrive, 0)
-        if ends_n:
-            take_tails(recvs[i], slice(LENGTHS[i] - 16, LENGTHS[i]), ends_n * BASE, 0)
-        past = 0 if ends_n else (f - MESSAGES[i - 1][0]) * BASE
+    def receive(i):
+        f, n, ends_at = MESSAGES[i]
+
+        all_messages(i).wait_recv()
+        if ends_at:
+            take_tails(recvs[i], slice(LENGTHS[i] - 16, LENGTHS[i]), len(ends_at) * BASE, 0)
+
+    def scale_message(i):
+        f, n, _ = MESSAGES[i]
 
         def base_step(slot, carry):
             layer, k = f + slot // BASE, lax.rem(slot, BASE)
             scale_block(
-                recvs[i], slot, tails[past + slot], layer * SLOTS + k, present(layer, k), out, scales
+                recvs[i], slot, tails[TAIL_AT[i] + slot], layer * SLOTS + k, present(layer, k), out, scales
             )
             return carry
 
@@ -551,20 +592,41 @@
 
         lax.fori_loop(0, LAYERS, place_step, 0)
 
+    def left_all(i):
+        all_messages(i).wait_send()
+
+    def halo_left():
+        for side in range(2):
+            @pl.when(has_next[side])
+            def _(side=side):
+                pltpu.make_async_remote_copy(
+                    src_ref=hsend.at[side],
+                    dst_ref=hrecv.at[side],
+                    send_sem=hs_sem.at[side],
+                    recv_sem=hr_sem.at[side, 0],
+                    device_id={"train": (right, left)[side]},
+                    device_id_type=MESH,
+                ).wait_send()
+
     def tell(step):
         return pltpu.make_async_remote_copy(
             src_ref=fsend,
             dst_ref=frecv.at[t],
-            send_sem=fs_sem.at[step],
-            recv_sem=fr_sem.at[step],
+            send_sem=fs_sem,
+            recv_sem=fr_sem,
             device_id={"train": lax.rem(t + step, TRAIN_N)},
             device_id_type=MESH,
         )
 
     pl.semaphore_wait(barrier, SERVE_N + TRAIN_N - 2)
-    for i in range(3):
-        for side in range(2):
-            halo(side, i).start()
+    for side in range(2):
+        @pl.when(has_next[side])
+        def _(side=side):
+            halo(side, 0).start()
+
+        @pl.when(jnp.logical_not(has_next[1 - side]))
+        def _(side=side):
+            hrecv[side] = jnp.zeros((EDGE, 128), BF)
     for copy in small:
         copy.wait()
     named[...] = jnp.full((16, 128), -1, I32)
@@ -606,6 +668,12 @@
     fsend[...] = jnp.broadcast_to(long, (8, 128))
     frecv[t] = fsend[...]
 
+    for side in range(2):
+        @pl.when(has_next[side])
+        def _(side=side):
+            halo(side, 1).start()
+            halo(side, 2).start()
+
     for step in range(1, TRAIN_N):
         tell(step).start()
     for copy in loads[2]:
@@ -615,46 +683,55 @@
     turn_tail(middle)
     lax.fori_loop(0, 1, prepare_step, 0)
     known.wait()
-    for side in range(2):
-        halo(side, 0).wait_recv()
+    halo_arrived(0)
     patch(0)
     dispatch(0)
     lax.fori_loop(1, PAIRS, prepare_step, 0, unroll=7)
-    for side in range(2):
-        halo(side, 1).wait_recv()
-        halo(side, 2).wait_recv()
+    halo_arrived(1)
+    halo_arrived(2)
     lax.fori_loop(1, PAIRS, patch_step, 0)
     dispatch_list()
     dispatch(1)
-    finish(0)
-    list_copy(0).wait_recv()
-    for i in range(4, 7):
+    for i in range(2):
+        list_copy(i).wait_recv()
+    for i in range(3, 6):
         list_copy(i).start()
     dispatch(2)
+    receive(0)
+    left_all(0)
+    receive(1)
+    scale_message(1)
+    list_copy(3).wait_recv()
+    list_copy(6).start()
     dispatch(3)
-    finish(1)
-    for i in range(1, 7):
-        list_copy(i).wait_recv()
+    dispatch(4)
+    left_all(1)
+    receive(2)
+    scale_message(2)
+    some_lists(4).wait_recv()
     list_copy(7).start()
+    left_all(2)
+    told = pltpu.make_async_remote_copy(
+        src_ref=frecv.at[0 : TRAIN_N - 1],
+        dst_ref=frecv.at[0 : TRAIN_N - 1],
+        send_sem=fs_sem,
+        recv_sem=fr_sem,
+        device_id={"train": right},
+        device_id_type=MESH,
+    )
+    told.wait_send()
+    told.wait_recv()
+    flag[...] = jnp.broadcast_to(jnp.max(frecv[...]).reshape(1, 1), (8, 128))
+    halo_left()
     finish_list()
-    finish(2)
-    finish(3)
-    for i in range(8):
-        list_copy(i).wait_send()
-    for step in range(1, TRAIN_N):
-        tell(step).wait()
-    flag[...] = jnp.broadcast_to(jnp.max(frecv[...]).reshape(1, 1), (8, 128))
-
-    for side in range(2):
-        halo(side, 0).wait_send()
-        halo(side, 1).wait_send()
-        halo(side, 2).wait_send()
-    for i in range(len(MESSAGES)):
-        def leave(j, carry, i=i):
-            message(i, j + 1).wait_send()
-            return carry
-
-        lax.fori_loop(0, SERVE_N - 1, leave, 0)
+    receive(3)
+    scale_message(3)
+    scale_message(0)
+    some_lists(15).wait_send()
+    receive(4)
+    scale_message(4)
+    left_all(3)
+    left_all(4)
 
 
 def everything(train_weights, row_offset, groups):
@@ -746,15 +823,15 @@
             pltpu.VMEM((SERVE_N, LIST, 128), BF),
             pltpu.SemaphoreType.DMA((2,)),
             pltpu.SemaphoreType.DMA,
-            pltpu.SemaphoreType.DMA((3, 3)),
+            pltpu.SemaphoreType.DMA((3, 2)),
+            pltpu.SemaphoreType.DMA((2,)),
             pltpu.SemaphoreType.DMA((2, 3)),
-            pltpu.SemaphoreType.DMA((2, 3)),
-            pltpu.SemaphoreType.DMA((parts, SERVE_N)),
-            pltpu.SemaphoreType.DMA((parts, SERVE_N)),
-            pltpu.SemaphoreType.DMA((8,)),
-            pltpu.SemaphoreType.DMA((8,)),
-            pltpu.SemaphoreType.DMA((TRAIN_N,)),
-            pltpu.SemaphoreType.DMA((TRAIN_N,)),
+            pltpu.SemaphoreType.DMA((parts,)),
+            pltpu.SemaphoreType.DMA((parts,)),
+            pltpu.SemaphoreType.DMA,
+            pltpu.SemaphoreType.DMA((5,)),
+            pltpu.SemaphoreType.DMA,
+            pltpu.SemaphoreType.DMA,
         ],
         compiler_params=pltpu.CompilerParams(
             collective_id=2, has_side_effects=True, vmem_limit_bytes=46 * 2**20

time: 78.4 us -> 73.1 us (0.932)
  Pallas kernels: 71.7 us -> 66.6 us
    pallas_call x1, Pallas kernels: 71.7 us -> 66.6 us  [shards(): pl.pallas_call(route, out_shape=(pltpu.VMEM((LAYERS * SLOTS, BLOCK, FEAT)...]
where the time goes in v2:
time: 73.1 us; the launch traced here: 72 us
  Pallas kernels  66.6 us (91%)
  local copies, waits for them, and re-layouts  4.1 us (6%)
  between operations  1.3 us (2%)
    pallas_call x1, Pallas kernels, shards(): pl.pallas_call(route, out_shape=(pltpu.VMEM((LAYERS * SLOTS, BLOCK, FEAT)...  66.6 us
    unnamed x2, local copies, waits for them, and re-layouts  3.59 us

profile of v2, /device:TPU:1, one launch (start us, length us, event | category | flops | bytes accessed | tf_op | source)
XLA Modules:
  0.0 72.0 jit_solution(4921609458187751190)
XLA Ops:
  0.6 66.6 %shard_map.50 = (bf16[48,32,2112]{2,1,0:T(8,128)(2,1)S(1)}, f32[48,1,2112]{2,1,0:T(1,128)S(1)}, f32[8,128]{1,0:T(8,128)S(1)}) custom-call(s32[16,28]{1,0:T(8,128)} %bitcast.18, s32[16,9]{1,0:T(8,128)} %offsets_in.1, bf16[132,16,960]{2,1,0:T(8,128)(2,1)} %bitcast.17), custom_call_target="tpu_custom_call" | custom-call | tf_op jit(solution)/shard_map/pallas_call | solution.py:792
  67.2 0.5 slice.3
  68.4 2.8 %copy.22 = bf16[16,1,1,3,32,2112]{5,4,3,2,1,0:T(8,128)(2,1)} copy(bf16[16,1,1,3,32,2112]{5,4,3,2,1,0:T(8,128)(2,1)S(1)} %get-tuple-element.60) | data formatting | bytes 12976128
  71.3 0.8 %copy.23 = f32[16,1,1,3,2112]{4,2,3,1,0:T(1,128)} copy(f32[16,1,1,3,2112]{4,2,3,1,0:T(1,128)S(1)} %get-tuple-element.61) | data formatting | bytes 811008
  (1 shorter events, 0.0 us)

commit v3 on v2

--- a/solution.py
+++ b/solution.py
@@ -465,6 +465,8 @@
 
         def send_step(j, carry):
             v = SERVE_N - 1 - j
+            turn = lax.rem(lax.rem(v // 2, 4) * (1 + 2 * mc), 4)
+            v = v // 8 * 8 + turn * 2 + lax.rem(v, 2)
             fill(sends[i], v, peer(v))
             message(i, v).start()
             return carry
@@ -482,7 +484,7 @@
             (pl.ds(list_of(0, 0), 1), 0, 3, 0),
             (pl.ds(list_of(0, 3), 1), 0, 1, 0),
             (pl.ds(list_of(1, 0), 1), 0, 1, 0),
-            (pl.ds(list_of(1, 0), 1), 0, 3, 0),
+            (pl.ds(list_of(0, 1), 1), 1, 0, 0),
             (pl.ds(list_of(0, 2), 1), 1, 0, 0),
             (pl.ds(8 * mc, 8), 0, 0, 1),
         )[i]
@@ -490,7 +492,7 @@
             src_ref=lists.at[lists_at],
             dst_ref=lists.at[lists_at],
             send_sem=ls_sem,
-            recv_sem=lr_sem.at[(0, 1, 4, 2, 4, 4, 4, 3)[i]],
+            recv_sem=lr_sem.at[(0, 1, 5, 2, 4, 4, 4, 3)[i]],
             device_id={"serve": peer(8 * dx + 2 * dy + dc)},
             device_id_type=MESH,
         )
@@ -692,7 +694,7 @@
     lax.fori_loop(1, PAIRS, patch_step, 0)
     dispatch_list()
     dispatch(1)
-    for i in range(2):
+    for i in range(3):
         list_copy(i).wait_recv()
     for i in range(3, 6):
         list_copy(i).start()
@@ -708,7 +710,7 @@
     left_all(1)
     receive(2)
     scale_message(2)
-    some_lists(4).wait_recv()
+    some_lists(3).wait_recv()
     list_copy(7).start()
     left_all(2)
     told = pltpu.make_async_remote_copy(
@@ -829,7 +831,7 @@
             pltpu.SemaphoreType.DMA((parts,)),
             pltpu.SemaphoreType.DMA((parts,)),
             pltpu.SemaphoreType.DMA,
-            pltpu.SemaphoreType.DMA((5,)),
+            pltpu.SemaphoreType.DMA((6,)),
             pltpu.SemaphoreType.DMA,
             pltpu.SemaphoreType.DMA,
         ],

time: 73.1 us -> 72.1 us (0.986)
  Pallas kernels: 66.6 us -> 65.5 us
    pallas_call x1, Pallas kernels: 66.6 us -> 65.5 us  [shards(): pl.pallas_call(route, out_shape=(pltpu.VMEM((LAYERS * SLOTS, BLOCK, FEAT)...]
where the time goes in v3:
time: 72.1 us; the launch traced here: 70.9 us
  Pallas kernels  65.5 us (91%)
  local copies, waits for them, and re-layouts  4.1 us (6%)
  between operations  1.3 us (2%)
    pallas_call x1, Pallas kernels, shards(): pl.pallas_call(route, out_shape=(pltpu.VMEM((LAYERS * SLOTS, BLOCK, FEAT)...  65.5 us
    unnamed x2, local copies, waits for them, and re-layouts  3.59 us

profile of v3, /device:TPU:1, one launch (start us, length us, event | category | flops | bytes accessed | tf_op | source)
XLA Modules:
  0.0 70.9 jit_solution(15629362972579123771)
XLA Ops:
  0.6 65.5 %shard_map.50 = (bf16[48,32,2112]{2,1,0:T(8,128)(2,1)S(1)}, f32[48,1,2112]{2,1,0:T(1,128)S(1)}, f32[8,128]{1,0:T(8,128)S(1)}) custom-call(s32[16,28]{1,0:T(8,128)} %bitcast.18, s32[16,9]{1,0:T(8,128)} %offsets_in.1, bf16[132,16,960]{2,1,0:T(8,128)(2,1)} %bitcast.17), custom_call_target="tpu_custom_call" | custom-call | tf_op jit(solution)/shard_map/pallas_call | solution.py:794
  66.1 0.5 slice.3
  67.3 2.8 %copy.22 = bf16[16,1,1,3,32,2112]{5,4,3,2,1,0:T(8,128)(2,1)} copy(bf16[16,1,1,3,32,2112]{5,4,3,2,1,0:T(8,128)(2,1)S(1)} %get-tuple-element.60) | data formatting | bytes 12976128
  70.1 0.8 %copy.23 = f32[16,1,1,3,2112]{4,2,3,1,0:T(1,128)} copy(f32[16,1,1,3,2112]{4,2,3,1,0:T(1,128)S(1)} %get-tuple-element.61) | data formatting | bytes 811008
  (1 shorter events, 0.0 us)

commit v4 on v3

--- a/solution.py
+++ b/solution.py
@@ -38,13 +38,15 @@
 MESSAGES = (
     (0, 2, ()),
     (2, 3, tuple(range(2, 10))),
-    (5, 5, ()),
-    (10, 4, tuple(range(10, 16)) + (0, 1)),
+    (5, 5, tuple(range(10, 16)) + (0, 1)),
+    (10, 4, ()),
     (14, 2, ()),
 )
 LENGTHS = tuple(n * BASE * BLOCK + (16 if m else 0) for _, n, m in MESSAGES)
+TILE_AT = {1: 0, 2: 16 + EXTRA}
 TAIL_AT = tuple(
-    next(m.index(f) * BASE for _, _, m in MESSAGES if f in m) for f, _, _ in MESSAGES
+    next(TILE_AT[i] + m.index(f) * BASE for i, (_, _, m) in enumerate(MESSAGES) if f in m)
+    for f, _, _ in MESSAGES
 )
 LIST = EXTRA * BLOCK + 16
 PAIRS = LAYERS // 2
@@ -561,7 +563,7 @@
 
         all_messages(i).wait_recv()
         if ends_at:
-            take_tails(recvs[i], slice(LENGTHS[i] - 16, LENGTHS[i]), len(ends_at) * BASE, 0)
+            take_tails(recvs[i], slice(LENGTHS[i] - 16, LENGTHS[i]), len(ends_at) * BASE, TILE_AT[i])
 
     def scale_message(i):
         f, n, _ = MESSAGES[i]
@@ -710,6 +712,7 @@
     left_all(1)
     receive(2)
     scale_message(2)
+    scale_message(0)
     some_lists(3).wait_recv()
     list_copy(7).start()
     left_all(2)
@@ -728,7 +731,6 @@
     finish_list()
     receive(3)
     scale_message(3)
-    scale_message(0)
     some_lists(15).wait_send()
     receive(4)
     scale_message(4)
@@ -816,7 +818,7 @@
             pltpu.VMEM((LAYERS * HELD, BLOCK, 128), BF),
             pltpu.VMEM((2, EDGE, 128), BF),
             pltpu.VMEM((2, EDGE, 128), BF),
-            pltpu.VMEM((16 + EXTRA, BLOCK, 128), F32),
+            pltpu.VMEM((32 + EXTRA, BLOCK, 128), F32),
             pltpu.VMEM((EXTRA, BLOCK, FEAT), BF),
             pltpu.VMEM((EXTRA, 1, FEAT), F32),
             pltpu.VMEM((8, 128), F32),

time: 72.1 us -> 72.5 us (level)
  the two profiles are of different devices: /device:TPU:1 before, /device:TPU:7 now
where the time goes in v4:
time: 72.5 us; the launch traced here: 72.4 us
  Pallas kernels  66.9 us (92%)
  local copies, waits for them, and re-layouts  4.1 us (6%)
  between operations  1.3 us (2%)
    pallas_call x1, Pallas kernels, shards(): pl.pallas_call(route, out_shape=(pltpu.VMEM((LAYERS * SLOTS, BLOCK, FEAT)...  66.9 us
    unnamed x2, local copies, waits for them, and re-layouts  3.59 us

profile of v4, /device:TPU:7, one launch (start us, length us, event | category | flops | bytes accessed | tf_op | source)
XLA Modules:
  0.0 72.4 jit_solution(7028621684735189211)
XLA Ops:
  0.6 66.9 %shard_map.50 = (bf16[48,32,2112]{2,1,0:T(8,128)(2,1)S(1)}, f32[48,1,2112]{2,1,0:T(1,128)S(1)}, f32[8,128]{1,0:T(8,128)S(1)}) custom-call(s32[16,28]{1,0:T(8,128)} %bitcast.18, s32[16,9]{1,0:T(8,128)} %offsets_in.1, bf16[132,16,960]{2,1,0:T(8,128)(2,1)} %bitcast.17), custom_call_target="tpu_custom_call" | custom-call | tf_op jit(solution)/shard_map/pallas_call | solution.py:796
  67.6 0.5 slice.3
  68.8 2.8 %copy.22 = bf16[16,1,1,3,32,2112]{5,4,3,2,1,0:T(8,128)(2,1)} copy(bf16[16,1,1,3,32,2112]{5,4,3,2,1,0:T(8,128)(2,1)S(1)} %get-tuple-element.60) | data formatting | bytes 12976128
  71.6 0.8 %copy.23 = f32[16,1,1,3,2112]{4,2,3,1,0:T(1,128)} copy(f32[16,1,1,3,2112]{4,2,3,1,0:T(1,128)S(1)} %get-tuple-element.61) | data formatting | bytes 811008
  (1 shorter events, 0.0 us)
